TPU v7x, 128 devices: a whole 4x4x4 slice. The times are simulated.
128 devices in a mesh: blk: 8 (over x, y_lo), uly: 2 (over core), dp: 8 (over z, y_hi).
Axes of the slice: x: 4, y: 4 (y_hi: 2, y_lo: 2; y = y_hi * 2 + y_lo), z: 4, core: 2. Of those that a mesh axis runs over, the one named last changes fastest.
Arguments:
- short_tokens: bfloat16 [64, 1024, 4096], P(('blk', 'dp'), 'uly'), may hold values from -150 to 150, as said below
- short_segments: int32 [64, 1024], P(('blk', 'dp')), may hold values from 0 to 3, never falling along the last dimension, each value on 1 to 512 neighbouring positions
- long_tokens: bfloat16 [8, 3072, 4096], P('dp', 'blk'), may hold values from -150 to 150, as said below
- long_lengths: int32 [8], P('dp'), may hold values from 768 to 3072
- w_query: bfloat16 [4096, 2048], P(('blk', 'dp'), 'uly'), may hold values from -0.09375 to 0.09375
- w_key: bfloat16 [4096, 512], P(('blk', 'dp'), 'uly'), may hold values from -0.09375 to 0.09375
- w_value: bfloat16 [4096, 512], P(('blk', 'dp'), 'uly'), may hold values from -0.09375 to 0.09375
Outputs:
- short_out: bfloat16 [64, 1024, 2048], P(('blk', 'dp'), 'uly')
- long_out: bfloat16 [8, 3072, 2048], P('dp', 'blk', 'uly')
Inputs may be any that keep to these rules, and one draw needn't show every extreme that they name: `short_tokens`: activations of the short bucket. `long_tokens`: activations of the long bucket; rows at or after a sequence's length are padding. `short_segments`: document numbers never fall along a sequence. `long_lengths`: a long sequence occupies positions 0 to its length - 1 of its 3072 slots.
All inputs are finite; a program needn't handle non-finite values.
Results may differ from a plain program's by a relative error of at most 0.012.
The roundings to bfloat16 on the way count: a program that leaves them out, or rounds other values in their place, can miss the bound.
Values may be sent and summed in bfloat16 or wider, within the bound.
No kernel may reach another device: no remote copies, remote signals or barrier semaphores. Data moves between devices by JAX's collectives and lax.ppermute only.
A program may use at most 128 MiB of HBM per device.

v0:
```python
import math

import jax
import jax.numpy as jnp
from jax import lax
from jax.sharding import PartitionSpec as P

HD = 128


masked_score = -1e30


def side_by_side(arrays, axis, dim, along):
    both = jnp.concatenate(arrays, axis=along)
    whole, at, outs = (lax.all_gather(both, axis, axis=dim, tiled=True), 0, [])
    for a in arrays:
        outs.append(lax.slice_in_dim(whole, at, at + a.shape[along], axis=along))
        at += a.shape[along]
    return tuple(outs)


def head_scores(query_rows, key_rows, kv_heads):
    query_heads = query_rows.reshape(query_rows.shape[0], kv_heads, -1, HD)
    key_heads = key_rows.reshape(key_rows.shape[0], kv_heads, HD)
    scores = jnp.einsum(
        "bhgd,khd->hgbk", query_heads, key_heads, preferred_element_type=jnp.float32
    )
    return scores * (1.0 / math.sqrt(HD))


def weighted_values(probabilities, value_rows, kv_heads):
    value_heads = value_rows.reshape(value_rows.shape[0], kv_heads, HD)
    return jnp.einsum(
        "hgbk,khd->hgbd", probabilities, value_heads, preferred_element_type=jnp.float32
    )


def short_attention(queries, key_rows, value_rows, segments):
    kv_heads = key_rows.shape[1] // HD
    seq_len = key_rows.shape[0]
    block_rows = min(512, seq_len)
    positions = jnp.arange(seq_len, dtype=jnp.int32)
    outputs = []
    for block_index in range(seq_len // block_rows):
        first_row = block_index * block_rows
        query_pos = positions[first_row : first_row + block_rows]
        query_seg = segments[first_row : first_row + block_rows]
        visible = (positions[None, :] <= query_pos[:, None]) & (
            segments[None, :] == query_seg[:, None]
        )
        scores = head_scores(queries[first_row : first_row + block_rows], key_rows, kv_heads)
        scores = jnp.where(visible, scores, masked_score)
        row_max = jnp.max(scores, axis=-1, keepdims=True)
        exponentials = jnp.where(visible, jnp.exp(scores - row_max), 0.0)
        totals = jnp.sum(exponentials, axis=-1)
        mixed = (
            weighted_values(exponentials.astype(jnp.bfloat16), value_rows, kv_heads)
            / totals[..., None]
        )
        outputs.append(jnp.transpose(mixed, (2, 0, 1, 3)).reshape(block_rows, -1))
    return jnp.concatenate(outputs, axis=0).astype(jnp.bfloat16)


def local(short_tokens, short_segments, long_tokens, long_lengths, w_query, w_key, w_value):
    short_rows = short_tokens[0]
    long_rows = long_tokens[0]
    long_count = long_rows.shape[0]
    query_cols = w_query.shape[1]
    kv_cols = w_key.shape[1]
    whole_rows = lax.all_gather(short_rows, "uly", axis=0, tiled=True)
    pieces = side_by_side((w_query, w_key, w_value), ("blk", "dp"), 0, 1)
    short_new = tuple(
        (jnp.dot(whole_rows, pieces[i], preferred_element_type=jnp.float32) for i in range(3))
    )
    long_new = tuple(
        (jnp.dot(long_rows, pieces[i], preferred_element_type=jnp.float32) for i in range(3))
    )
    projected = short_new + long_new
    query_short, key_short, value_short = tuple(
        (item.astype(jnp.bfloat16) for item in projected[:3])
    )
    query_long, key_long, value_long = tuple((item.astype(jnp.bfloat16) for item in projected[3:]))
    attended = short_attention(query_short, key_short, value_short, short_segments[0])
    short_back = lax.all_to_all(attended, "uly", split_axis=0, concat_axis=1, tiled=True)
    long_len = long_lengths[0]
    query_pos = lax.axis_index("blk") * long_count + jnp.arange(long_count, dtype=jnp.int32)
    kv_heads = kv_cols // HD
    group_size = query_cols // kv_cols
    cycle_init = (
        jnp.full((kv_heads, group_size, long_count), masked_score, jnp.float32),
        jnp.zeros((kv_heads, group_size, long_count), jnp.float32),
        jnp.zeros((kv_heads, group_size, long_count, HD), jnp.float32),
    )
    carry = cycle_init
    key_piece, value_piece = side_by_side((key_long, value_long), "blk", 0, 1)
    piece_rows = key_piece.shape[0]
    block_rows = math.gcd(piece_rows, 512)
    blocks_count = piece_rows // block_rows
    key_blocks = key_piece.reshape(blocks_count, block_rows, -1)
    value_blocks = value_piece.reshape(blocks_count, block_rows, -1)
    block_starts = block_rows * jnp.arange(blocks_count, dtype=jnp.int32)

    def update(states, block_key, block_value, block_start):
        running_max, running_sum, accumulated = states
        key_pos = block_start + jnp.arange(block_rows, dtype=jnp.int32)
        visible = (key_pos[None, :] <= query_pos[:, None]) & (key_pos[None, :] < long_len)
        scores = jnp.where(visible, head_scores(query_long, block_key, kv_heads), masked_score)
        new_max = jnp.maximum(running_max, jnp.max(scores, axis=-1))
        rescale = jnp.exp(running_max - new_max)
        exponentials = jnp.where(visible, jnp.exp(scores - new_max[..., None]), 0.0)
        running_sum = running_sum * rescale + jnp.sum(exponentials, axis=-1)
        accumulated = accumulated * rescale[..., None] + weighted_values(
            exponentials.astype(jnp.bfloat16), block_value, kv_heads
        )
        return (new_max, running_sum, accumulated)

    def advance(states, inputs):
        block_key, block_value, block_start = inputs
        needed = (block_start <= query_pos[-1]) & (block_start < long_len)
        states = lax.cond(
            needed,
            lambda current: update(current, block_key, block_value, block_start),
            lambda current: current,
            states,
        )
        return (states, None)

    carry, unused = lax.scan(advance, carry, (key_blocks, value_blocks, block_starts))
    running_max, running_sum, accumulated = carry
    mixed = accumulated / running_sum[..., None]
    mixed = jnp.transpose(mixed, (2, 0, 1, 3)).reshape(long_count, query_cols)
    mixed = jnp.where(query_pos[:, None] < long_len, mixed, 0.0)
    return (short_back[None], mixed.astype(jnp.bfloat16)[None])


def solution(mesh):
    return jax.shard_map(
        local,
        mesh=mesh,
        in_specs=(
            P(("blk", "dp"), "uly", None),
            P(("blk", "dp"), None),
            P("dp", "blk", None),
            P("dp"),
            P(("blk", "dp"), "uly"),
            P(("blk", "dp"), "uly"),
            P(("blk", "dp"), "uly"),
        ),
        out_specs=(P(("blk", "dp"), "uly", None), P("dp", "blk", "uly")),
        check_vma=False,
    )
```

profile of v0, /device:TPU:71, one launch (start us, length us, event | category | flops | bytes accessed | tf_op | source)
XLA Modules:
  0.0 606.0 jit_solution(7188982247814746928)
XLA Ops:
  11.3 2.6 fusion.47
  13.9 300.1 %all-gather.5.cloned.1.call-done = bf16[4096,1536]{1,0:T(8,128)(2,1)} async-done(((bf16[64,1536]{1,0:T(8,128)(2,1)}), bf16[4096,1536]{1,0:T(8,128)(2,1)}) %all-gather.5.cloned.1.call-update) | async-done | bytes 12582928 | tf_op jit(solution)/shard_map/all_gather | solution.py:16
  314.0 2.9 fusion.91
  316.9 2.9 fusion.96
  320.6 74.6 %all-gather.9.cloned.1.call-done = bf16[1,1024,4096]{2,1,0:T(8,128)(2,1)} async-done(((bf16[1,512,4096]{2,1,0:T(8,128)(2,1)}), bf16[1,1024,4096]{2,1,0:T(8,128)(2,1)}) %all-gather.9.cloned.1.call-update) | async-done | bytes 8388624 | tf_op jit(solution)/shard_map/all_gather | solution.py:71
  395.2 7.4 %fusion.76 = bf16[256,1024]{1,0:T(8,128)(2,1)} fusion(bf16[1,1024,4096]{2,1,0:T(8,128)(2,1)} %all-gather.9.cloned.1.call-done, bf16[4096,1536]{1,0:T(8,128)(2,1)} %all-gather.5.cloned.1.call-done), kind=kOutput, calls=%fused_computation.73 | convolution fusion | flops 2147745792 | bytes 11010048 | tf_op jit(solution)/shard_map/dot_general | solution.py:74
  402.6 11.5 %convert_bitcast_fusion = bf16[1024,1024]{0,1:T(8,128)(2,1)S(1)} fusion(bf16[1,1024,4096]{2,1,0:T(8,128)(2,1)S(1)} %copy-done.3, bf16[4096,1536]{1,0:T(8,128)(2,1)} %all-gather.5.cloned.1.call-done), kind=kOutput, calls=%fused_computation.60 | convolution fusion | flops 8590983168 | bytes 18874368 | tf_op jit(solution)/shard_map/dot_general | solution.py:74
  414.1 5.0 fusion.71
  420.6 12.3 %fusion.108 = (f32[2,4,512]{2,1,0:T(4,128)S(1)}, bf16[2,4,512,1024]{2,3,1,0:T(8,128)(2,1)}) fusion(bf16[1024,2,128,1]{0,2,3,1:T(8,128)(2,1)} %bitcast.174, bf16[512,2,4,128]{0,3,2,1:T(8,128)(2,1)} %bitcast.164, pred[512,1024]{0,1:T(8,128)(4,1)} %get-tuple-element.220), kind=kOutput, calls=%fused_computation.90 | convolution fusion | flops 1098908672 | bytes 10502144 | tf_op jit(solution)/shard_map/sub | solution.py:55
  432.9 5.9 fusion.45
  438.8 12.1 %fusion.109 = (f32[2,4,512]{2,1,0:T(4,128)S(1)}, bf16[2,4,512,1024]{2,3,1,0:T(8,128)(2,1)}) fusion(bf16[1024,2,128,1]{0,2,3,1:T(8,128)(2,1)} %bitcast.175, bf16[512,2,4,128]{0,3,2,1:T(8,128)(2,1)} %bitcast.162, pred[512,1024]{0,1:T(8,128)(4,1)} %get-tuple-element.219), kind=kOutput, calls=%fused_computation.91 | convolution fusion | flops 1098908672 | bytes 10502144 | tf_op jit(solution)/shard_map/sub | solution.py:55
  450.9 5.0 fusion.46
  457.5 4.0 copy.66
  461.4 8.6 %all_to_all.13 = bf16[2,512,1024]{2,1,0:T(8,128)(2,1)} all-to-all(bf16[2,512,1024]{2,1,0:T(8,128)(2,1)} %bitcast.154), channel_id=1, replica_groups=mesh['blk'=8,'uly'=2,'dp'=8] {'uly'}, dimensions={0} | all-to-all | bytes 4194304 | tf_op jit(solution)/shard_map/all_to_all | solution.py:85
  470.0 4.0 copy.67
  474.0 3.9 copy.74
  477.9 7.9 %fusion.66 = bf16[384,1024]{0,1:T(8,128)(2,1)} fusion(bf16[1,384,4096]{2,1,0:T(8,128)(2,1)S(1)} %copy-done, bf16[4096,1536]{1,0:T(8,128)(2,1)} %all-gather.5.cloned.1.call-done), kind=kOutput, calls=%fused_computation.71 | convolution fusion | flops 3221618688 | bytes 12320768 | tf_op jit(solution)/shard_map/dot_general | solution.py:77
  487.2 3.7 fusion.105
  498.9 92.0 %while.14 = (s32[]{:T(128)}, f32[2,4,384]{2,1,0:T(4,128)S(1)}, f32[2,4,384]{2,1,0:T(4,128)S(1)}, f32[2,4,384,128]{3,2,1,0:T(8,128)}, s32[6]{0:T(128)S(1)}, /*ind...) while((s32[]{:T(128)}, f32[2,4,384]{2,1,0:T(4,128)S(1)}, ...), condition=%wide.region_9.10_spmd, body=%wide.region_4.9_spmd.sunk | while | flops 826940928 | bytes 26942268 | solution.py:129
  502.7 11.5 %conditional.2 = ((f32[2,4,384]{2,1,0:T(4,128)S(1)}, f32[2,4,384]{2,1,0:T(4,128)S(1)}, f32[2,4,384,128]{3,2,1,0:T(8,128)})) conditional(s32[]{:T(128)} %convert_element_type.107, (f32[2,4,384]{2,1,0:T(4,128)S(1)}, f32[2,4,384]{2,1,0:T(4,128)S(1)}, f32[2,4,384,128]{3,2,1,0:T(8,128)}) %tuple.52, (s32[]{:T(128)}, s32[384]{0:T(512)S(1)}, s32[]{:T(128)}, ...), branch_computations={%region_5.5_spmd, %region_6.8_spmd} | conditional | flops 826940928 | bytes 26942000 | solution.py:121
  509.5 4.7 multiply_add_fusion
  518.0 11.5 %conditional.2 = ((f32[2,4,384]{2,1,0:T(4,128)S(1)}, f32[2,4,384]{2,1,0:T(4,128)S(1)}, f32[2,4,384,128]{3,2,1,0:T(8,128)})) conditional(s32[]{:T(128)} %convert_element_type.107, (f32[2,4,384]{2,1,0:T(4,128)S(1)}, f32[2,4,384]{2,1,0:T(4,128)S(1)}, f32[2,4,384,128]{3,2,1,0:T(8,128)}) %tuple.52, (s32[]{:T(128)}, s32[384]{0:T(512)S(1)}, s32[]{:T(128)}, ...), branch_computations={%region_5.5_spmd, %region_6.8_spmd} | conditional | flops 826940928 | bytes 26942000 | solution.py:121
  524.8 4.7 multiply_add_fusion
  533.3 11.5 %conditional.2 = ((f32[2,4,384]{2,1,0:T(4,128)S(1)}, f32[2,4,384]{2,1,0:T(4,128)S(1)}, f32[2,4,384,128]{3,2,1,0:T(8,128)})) conditional(s32[]{:T(128)} %convert_element_type.107, (f32[2,4,384]{2,1,0:T(4,128)S(1)}, f32[2,4,384]{2,1,0:T(4,128)S(1)}, f32[2,4,384,128]{3,2,1,0:T(8,128)}) %tuple.52, (s32[]{:T(128)}, s32[384]{0:T(512)S(1)}, s32[]{:T(128)}, ...), branch_computations={%region_5.5_spmd, %region_6.8_spmd} | conditional | flops 826940928 | bytes 26942000 | solution.py:121
  540.1 4.7 multiply_add_fusion
  548.7 11.5 %conditional.2 = ((f32[2,4,384]{2,1,0:T(4,128)S(1)}, f32[2,4,384]{2,1,0:T(4,128)S(1)}, f32[2,4,384,128]{3,2,1,0:T(8,128)})) conditional(s32[]{:T(128)} %convert_element_type.107, (f32[2,4,384]{2,1,0:T(4,128)S(1)}, f32[2,4,384]{2,1,0:T(4,128)S(1)}, f32[2,4,384,128]{3,2,1,0:T(8,128)}) %tuple.52, (s32[]{:T(128)}, s32[384]{0:T(512)S(1)}, s32[]{:T(128)}, ...), branch_computations={%region_5.5_spmd, %region_6.8_spmd} | conditional | flops 826940928 | bytes 26942000 | solution.py:121
  555.5 4.7 multiply_add_fusion
  564.0 11.5 %conditional.2 = ((f32[2,4,384]{2,1,0:T(4,128)S(1)}, f32[2,4,384]{2,1,0:T(4,128)S(1)}, f32[2,4,384,128]{3,2,1,0:T(8,128)})) conditional(s32[]{:T(128)} %convert_element_type.107, (f32[2,4,384]{2,1,0:T(4,128)S(1)}, f32[2,4,384]{2,1,0:T(4,128)S(1)}, f32[2,4,384,128]{3,2,1,0:T(8,128)}) %tuple.52, (s32[]{:T(128)}, s32[384]{0:T(512)S(1)}, s32[]{:T(128)}, ...), branch_computations={%region_5.5_spmd, %region_6.8_spmd} | conditional | flops 826940928 | bytes 26942000 | solution.py:121
  570.8 4.7 multiply_add_fusion
  579.4 11.5 %conditional.2 = ((f32[2,4,384]{2,1,0:T(4,128)S(1)}, f32[2,4,384]{2,1,0:T(4,128)S(1)}, f32[2,4,384,128]{3,2,1,0:T(8,128)})) conditional(s32[]{:T(128)} %convert_element_type.107, (f32[2,4,384]{2,1,0:T(4,128)S(1)}, f32[2,4,384]{2,1,0:T(4,128)S(1)}, f32[2,4,384,128]{3,2,1,0:T(8,128)}) %tuple.52, (s32[]{:T(128)}, s32[384]{0:T(512)S(1)}, s32[]{:T(128)}, ...), branch_computations={%region_5.5_spmd, %region_6.8_spmd} | conditional | flops 826940928 | bytes 26942000 | solution.py:121
  586.2 4.7 multiply_add_fusion
  594.4 2.3 reshape.130
  (110 shorter events, 70.0 us)
Async XLA Ops:
  7.2 306.8 %copy-start = (bf16[1,384,4096]{2,1,0:T(8,128)(2,1)S(1)}, bf16[1,384,4096]{2,1,0:T(8,128)(2,1)}, u32[]{:S(2)}) copy-start(bf16[1,384,4096]{2,1,0:T(8,128)(2,1)} %param.13) | copy-start | bytes 9437188
  7.2 306.8 %all-gather.5.cloned.1.call-start = ((), (), s32[]{:S(2)}) async-start(), calls=%async_computation.1 | async-start | bytes 12779520 | tf_op jit(solution)/shard_map/all_gather | solution.py:16
  9.0 386.2 %all-gather.9.cloned.1.call-start = ((), (), s32[]{:S(2)}) async-start(), calls=%async_computation.3 | async-start | bytes 12582912 | tf_op jit(solution)/shard_map/all_gather | solution.py:71
  9.8 477.4 %all-gather.7.cloned.1.call-start = ((), (), s32[]{:S(2)}) async-start(), calls=%async_computation.2 | async-start | bytes 3538944 | tf_op jit(solution)/shard_map/all_gather | solution.py:16
  395.2 7.4 %copy-start.3 = (bf16[1,1024,4096]{2,1,0:T(8,128)(2,1)S(1)}, bf16[1,1024,4096]{2,1,0:T(8,128)(2,1)}, u32[]{:S(2)}) copy-start(bf16[1,1024,4096]{2,1,0:T(8,128)(2,1)} %all-gather.9.cloned.1.call-done) | copy-start | bytes 25165828
  450.9 5.0 copy-start.2
  590.9 8.1 %copy-start.1 = (bf16[1,384,4096]{2,1,0:T(8,128)(2,1)S(1)}, bf16[1,384,4096]{2,1,0:T(8,128)(2,1)}, u32[]{:S(2)}) copy-start(bf16[1,384,4096]{2,1,0:T(8,128)(2,1)} %param.13) | copy-start | bytes 9437188
Sparse Core Ops, SparseCore 0:
  10.2 303.7 all-gather.4
  315.6 79.5 all-gather.8
  396.9 70.6 all-gather.6
where the time goes:
time: 613 us; the launch traced here: 606 us
  waiting for transfers between devices  375 us (61%)
  matrix products  109 us (18%)
  local copies, waits for them, and re-layouts  48 us (8%)
  other arithmetic  33.8 us (6%)
  loops' own time  15.9 us (3%)
  between operations  15 us (2%)
  blocking collectives  8.59 us (1%)
    all_gather x2, waiting for transfers between devices, side_by_side(): whole, at, outs = (lax.all_gather(both, axis, axis=dim, tiled=True), 0, [])  300 us
    all_gather x1, waiting for transfers between devices, local(): whole_rows = lax.all_gather(short_rows, 'uly', axis=0, tiled=True)  74.6 us
    dot_general x8, matrix products, weighted_values(): jnp.einsum('hgbk,khd->hgbd', probabilities, value_heads, preferred_elemen...  39.2 us
    sub x2, matrix products, short_attention(): exponentials = jnp.where(visible, jnp.exp(scores - row_max), 0.0)  24.5 us
    dot_general x3, matrix products, local(): jnp.dot(whole_rows, pieces[i], preferred_element_type=jnp.float32)  23.8 us
    another operation x1, loops' own time, local(): lax.scan(advance, carry, (key_blocks, value_blocks, block_starts))  15.5 us
    dot_general x3, matrix products, local(): jnp.dot(long_rows, pieces[i], preferred_element_type=jnp.float32)  13.7 us
  transfers between devices with their start and end apart: 3, of which 2 were waited for; matrix products, arithmetic and copies ran while one was open for 15% of the time, Pallas kernels for 0%

commit v1 on v0

--- a/solution.py
+++ b/solution.py
@@ -9,6 +9,27 @@
 
 
 masked_score = -1e30
+
+
+def torus_order():
+    return [
+        (x * 2 + y % 2) * 8 + z * 2 + y // 2 for x in range(4) for z in range(4) for y in range(4)
+    ]
+
+
+def gathered_weights(arrays):
+    both = jnp.concatenate(arrays, axis=1)
+    whole = lax.all_gather(
+        both, ("blk", "dp"), axis=0, tiled=True, axis_index_groups=[torus_order()]
+    )
+    rows = both.shape[0]
+    whole = whole.reshape(4, 4, 2, 2, rows, both.shape[1])
+    whole = jnp.transpose(whole, (0, 3, 1, 2, 4, 5)).reshape(64 * rows, both.shape[1])
+    at, outs = 0, []
+    for a in arrays:
+        outs.append(lax.slice_in_dim(whole, at, at + a.shape[1], axis=1))
+        at += a.shape[1]
+    return tuple(outs)
 
 
 def side_by_side(arrays, axis, dim, along):
@@ -68,8 +89,12 @@
     long_count = long_rows.shape[0]
     query_cols = w_query.shape[1]
     kv_cols = w_key.shape[1]
-    whole_rows = lax.all_gather(short_rows, "uly", axis=0, tiled=True)
-    pieces = side_by_side((w_query, w_key, w_value), ("blk", "dp"), 0, 1)
+    partner_rows = lax.ppermute(short_rows, "uly", [(0, 1), (1, 0)])
+    first = lax.axis_index("uly") == 0
+    whole_rows = jnp.concatenate(
+        [jnp.where(first, short_rows, partner_rows), jnp.where(first, partner_rows, short_rows)]
+    )
+    pieces = gathered_weights((w_query, w_key, w_value))
     short_new = tuple(
         (jnp.dot(whole_rows, pieces[i], preferred_element_type=jnp.float32) for i in range(3))
     )

time: 613 us -> 375 us (0.61)
  the two profiles are of different devices: /device:TPU:71 before, /device:TPU:63 now
where the time goes in v1:
time: 375 us; the launch traced here: 368 us
  matrix products  108 us (29%)
  local copies, waits for them, and re-layouts  87.8 us (23%)
  waiting for transfers between devices  82.9 us (22%)
  other arithmetic  38.7 us (10%)
  blocking collectives  18.8 us (5%)
  loops' own time  16.1 us (4%)
  between operations  15 us (4%)
    all_gather x1, waiting for transfers between devices, gathered_weights(): lax.all_gather(both, ('blk', 'dp'), axis=0, tiled=True, axis_index_groups...  79.8 us
    dot_general x3, matrix products, local(): jnp.dot(whole_rows, pieces[i], preferred_element_type=jnp.float32)  28 us
    dot_general x8, matrix products, weighted_values(): jnp.einsum('hgbk,khd->hgbd', probabilities, value_heads, preferred_elemen...  27 us
    sub x2, matrix products, short_attention(): exponentials = jnp.where(visible, jnp.exp(scores - row_max), 0.0)  24.5 us
    all_to_all x1, blocking collectives, local(): lax.all_to_all(attended, 'uly', split_axis=0, concat_axis=1, tiled=True)  18.8 us
    reshape x6, local copies, waits for them, and re-layouts, head_scores(): query_heads = query_rows.reshape(query_rows.shape[0], kv_heads, -1, HD)  15.8 us
    another operation x1, loops' own time, local(): lax.scan(advance, carry, (key_blocks, value_blocks, block_starts))  15.4 us
    dot_general x6, matrix products, head_scores(): jnp.einsum('bhgd,khd->hgbk', query_heads, key_heads, preferred_element_ty...  15.1 us
  transfers between devices with their start and end apart: 3, of which 2 were waited for; matrix products, arithmetic and copies ran while one was open for 20% of the time, Pallas kernels for 0%

profile of v1, /device:TPU:63, one launch (start us, length us, event | category | flops | bytes accessed | tf_op | source)
XLA Modules:
  0.0 368.4 jit_solution(16446771256020380388)
XLA Ops:
  13.9 3.1 collective-permute-done
  17.0 5.8 %broadcast_select_fusion.1 = (bf16[512,4096]{1,0:T(8,128)(2,1)}, bf16[512,4096]{1,0:T(8,128)(2,1)}) fusion(bf16[512,4096]{1,0:T(8,128)(2,1)} %collective-permute-done, pred[]{:T(512)S(6)} %eq.38, bf16[1,512,4096]{2,1,0:T(8,128)(2,1)} %param.11), kind=kLoop, calls=%fused_computation.46 | loop fusion | flops 4194304 | bytes 16777216 | tf_op jit(solution)/shard_map/jit(_where)/select_n | solution.py:95
  22.7 79.8 %all-gather.3.cloned.1.call-done = bf16[4096,1536]{1,0:T(8,128)(2,1)} async-done(((bf16[64,1536]{1,0:T(8,128)(2,1)}), bf16[4096,1536]{1,0:T(8,128)(2,1)}) %all-gather.3.cloned.1.call-update) | async-done | bytes 12582928 | tf_op jit(solution)/shard_map/all_gather | solution.py:22
  102.5 6.5 %copy.79 = bf16[4,2,4,2,64,1536]{5,4,3,2,1,0:T(8,128)(2,1)S(1)} copy(bf16[4,2,4,2,64,1536]{5,4,1,3,2,0:T(8,128)(2,1)} %bitcast.142) | data formatting | bytes 25165824 | tf_op jit(solution)/shard_map/transpose | solution.py:27
  108.9 4.5 %copy-done.1 = bf16[4,2,4,2,64,1536]{5,4,3,2,1,0:T(8,128)(2,1)} copy-done((bf16[4,2,4,2,64,1536]{5,4,3,2,1,0:T(8,128)(2,1)}, bf16[4,2,4,2,64,1536]{5,4,3,2,1,0:T(8,128)(2,1)S(1)}, u32[]{:S(2)}) %copy-start.1) | copy-done | bytes 12582936
  113.5 5.7 %fusion.70 = bf16[1024,256]{0,1:T(8,128)(2,1)} fusion(bf16[4096,1536]{1,0:T(8,128)(2,1)S(1)} %bitcast.143, bf16[512,4096]{1,0:T(8,128)(2,1)} %get-tuple-element.226, bf16[512,4096]{1,0:T(8,128)(2,1)} %get-tuple-element.225), kind=kOutput, calls=%fused_computation.73 | convolution fusion | flops 2164523008 | bytes 11010048 | tf_op jit(solution)/shard_map/dot_general | solution.py:99
  119.2 15.0 %fusion.46 = bf16[1024,1024]{0,1:T(8,128)(2,1)} fusion(bf16[4096,1536]{1,0:T(8,128)(2,1)} %bitcast.144, bf16[512,4096]{1,0:T(8,128)(2,1)} %get-tuple-element.226, bf16[512,4096]{1,0:T(8,128)(2,1)} %get-tuple-element.225), kind=kOutput, calls=%fused_computation.63 | convolution fusion | flops 8607760384 | bytes 18874368 | tf_op jit(solution)/shard_map/dot_general | solution.py:99
  134.3 2.9 fusion.83
  137.2 3.0 fusion.88
  142.5 7.2 %fusion.67 = bf16[1024,256]{0,1:T(8,128)(2,1)} fusion(bf16[4096,1536]{1,0:T(8,128)(2,1)} %bitcast.147, bf16[512,4096]{1,0:T(8,128)(2,1)} %get-tuple-element.226, bf16[512,4096]{1,0:T(8,128)(2,1)} %get-tuple-element.225), kind=kOutput, calls=%fused_computation.72 | convolution fusion | flops 2164523008 | bytes 11010048 | tf_op jit(solution)/shard_map/dot_general | solution.py:99
  149.7 12.4 %fusion.103 = (f32[2,4,512]{2,1,0:T(4,128)S(1)}, bf16[2,4,512,1024]{2,3,1,0:T(8,128)(2,1)}) fusion(bf16[1024,2,128,1]{0,2,3,1:T(8,128)(2,1)} %bitcast.170, bf16[512,2,4,128]{0,3,2,1:T(8,128)(2,1)} %bitcast.159, pred[512,1024]{0,1:T(8,128)(4,1)} %get-tuple-element.232), kind=kOutput, calls=%fused_computation.93 | convolution fusion | flops 1098908672 | bytes 10502144 | tf_op jit(solution)/shard_map/sub | solution.py:76
  162.1 5.9 %fusion.42 = bf16[512,2,4,128]{0,3,2,1:T(8,128)(2,1)} fusion(bf16[1024,2,128,1]{0,2,3,1:T(8,128)(2,1)} %bitcast.168, bf16[2,4,512,1024]{2,3,1,0:T(8,128)(2,1)} %get-tuple-element.236, f32[512,2,4]{0,2,1:T(4,128)S(1)} %bitcast.173), kind=kOutput, calls=%fused_computation.56 | convolution fusion | flops 1074790400 | bytes 9977856 | tf_op jit(solution)/shard_map/hgbk,khd->hgbd/dot_general | solution.py:55
  168.1 12.2 %fusion.104 = (f32[2,4,512]{2,1,0:T(4,128)S(1)}, bf16[2,4,512,1024]{2,3,1,0:T(8,128)(2,1)}) fusion(bf16[1024,2,128,1]{0,2,3,1:T(8,128)(2,1)} %bitcast.171, bf16[512,2,4,128]{0,3,2,1:T(8,128)(2,1)} %bitcast.158, pred[512,1024]{0,1:T(8,128)(4,1)} %get-tuple-element.231), kind=kOutput, calls=%fused_computation.94 | convolution fusion | flops 1098908672 | bytes 10502144 | tf_op jit(solution)/shard_map/sub | solution.py:76
  180.2 5.0 %fusion.43 = bf16[512,2,4,128]{0,3,2,1:T(8,128)(2,1)S(1)} fusion(bf16[1024,2,128,1]{0,2,3,1:T(8,128)(2,1)} %bitcast.169, bf16[2,4,512,1024]{2,3,1,0:T(8,128)(2,1)} %get-tuple-element.238, f32[512,2,4]{0,2,1:T(4,128)S(1)} %bitcast.172), kind=kOutput, calls=%fused_computation.58 | convolution fusion | flops 1074790400 | bytes 9977856 | tf_op jit(solution)/shard_map/hgbk,khd->hgbd/dot_general | solution.py:55
  186.8 4.0 %copy.86 = bf16[1024,1024]{1,0:T(8,128)(2,1)} copy(bf16[1024,1024]{0,1:T(8,128)(2,1)} %pad_maximum_fusion.4) | data formatting | bytes 4194304 | tf_op jit(solution)/shard_map/concatenate | solution.py:83
  190.7 18.8 %all_to_all.13 = bf16[2,512,1024]{2,1,0:T(8,128)(2,1)} all-to-all(bf16[2,512,1024]{2,1,0:T(8,128)(2,1)} %bitcast.149), channel_id=1, replica_groups=mesh['blk'=8,'uly'=2,'dp'=8] {'uly'}, dimensions={0} | all-to-all | bytes 4194304 | tf_op jit(solution)/shard_map/all_to_all | solution.py:110
  209.5 4.0 %copy.87 = bf16[2,512,1024]{1,2,0:T(8,128)(2,1)} copy(bf16[2,512,1024]{2,1,0:T(8,128)(2,1)} %all_to_all.13) | data formatting | bytes 4194304 | tf_op jit(solution)/shard_map/all_to_all | solution.py:110
  213.5 3.9 %copy.94 = bf16[1,512,2048]{2,1,0:T(8,128)(2,1)} copy(bf16[1,512,2048]{1,2,0:T(8,128)(2,1)} %bitcast.150) | data formatting | bytes 4194304
  217.4 7.9 %fusion.62 = bf16[384,1024]{0,1:T(8,128)(2,1)} fusion(bf16[1,384,4096]{2,1,0:T(8,128)(2,1)S(1)} %copy-done, bf16[4096,1536]{1,0:T(8,128)(2,1)} %bitcast.148), kind=kOutput, calls=%fused_computation.71 | convolution fusion | flops 3221618688 | bytes 12320768 | tf_op jit(solution)/shard_map/dot_general | solution.py:102
  227.6 3.7 %fusion.100 = (bf16[3072,256]{0,1:T(8,128)(2,1)}, bf16[3072,256]{0,1:T(8,128)(2,1)}) fusion(bf16[3072,512]{0,1:T(8,128)(2,1)} %all-gather.5.cloned.1.call-done), kind=kLoop, calls=%fused_computation.90 | loop fusion | bytes 6291456 | tf_op jit(solution)/shard_map/slice | solution.py:39
  243.0 110.5 %while.14 = (s32[]{:T(128)}, f32[2,4,384]{2,1,0:T(4,128)S(1)}, f32[2,4,384]{2,1,0:T(4,128)S(1)}, f32[2,4,384,128]{3,2,1,0:T(8,128)}, s32[6]{0:T(128)S(1)}, /*ind...) while((s32[]{:T(128)}, f32[2,4,384]{2,1,0:T(4,128)S(1)}, ...), condition=%wide.region_9.10_spmd, body=%wide.region_4.9_spmd.sunk | while | flops 826940928 | bytes 40573840 | solution.py:154
  246.8 14.7 %conditional.2 = ((f32[2,4,384]{2,1,0:T(4,128)S(1)}, f32[2,4,384]{2,1,0:T(4,128)S(1)}, f32[2,4,384,128]{3,2,1,0:T(8,128)})) conditional(s32[]{:T(128)} %convert_element_type.95, (f32[2,4,384]{2,1,0:T(4,128)S(1)}, f32[2,4,384]{2,1,0:T(4,128)S(1)}, f32[2,4,384,128]{3,2,1,0:T(8,128)}) %tuple.54, (s32[]{:T(128)}, s32[384]{0:T(512)S(1)}, s32[]{:T(128)}, ...), branch_computations={%region_5.5_spmd, %region_6.8_spmd} | conditional | flops 826940928 | bytes 40573572 | solution.py:146
  257.6 2.7 multiply_add_fusion
  265.2 14.7 %conditional.2 = ((f32[2,4,384]{2,1,0:T(4,128)S(1)}, f32[2,4,384]{2,1,0:T(4,128)S(1)}, f32[2,4,384,128]{3,2,1,0:T(8,128)})) conditional(s32[]{:T(128)} %convert_element_type.95, (f32[2,4,384]{2,1,0:T(4,128)S(1)}, f32[2,4,384]{2,1,0:T(4,128)S(1)}, f32[2,4,384,128]{3,2,1,0:T(8,128)}) %tuple.54, (s32[]{:T(128)}, s32[384]{0:T(512)S(1)}, s32[]{:T(128)}, ...), branch_computations={%region_5.5_spmd, %region_6.8_spmd} | conditional | flops 826940928 | bytes 40573572 | solution.py:146
  276.0 2.7 multiply_add_fusion
  283.6 14.7 %conditional.2 = ((f32[2,4,384]{2,1,0:T(4,128)S(1)}, f32[2,4,384]{2,1,0:T(4,128)S(1)}, f32[2,4,384,128]{3,2,1,0:T(8,128)})) conditional(s32[]{:T(128)} %convert_element_type.95, (f32[2,4,384]{2,1,0:T(4,128)S(1)}, f32[2,4,384]{2,1,0:T(4,128)S(1)}, f32[2,4,384,128]{3,2,1,0:T(8,128)}) %tuple.54, (s32[]{:T(128)}, s32[384]{0:T(512)S(1)}, s32[]{:T(128)}, ...), branch_computations={%region_5.5_spmd, %region_6.8_spmd} | conditional | flops 826940928 | bytes 40573572 | solution.py:146
  294.4 2.7 multiply_add_fusion
  302.0 14.7 %conditional.2 = ((f32[2,4,384]{2,1,0:T(4,128)S(1)}, f32[2,4,384]{2,1,0:T(4,128)S(1)}, f32[2,4,384,128]{3,2,1,0:T(8,128)})) conditional(s32[]{:T(128)} %convert_element_type.95, (f32[2,4,384]{2,1,0:T(4,128)S(1)}, f32[2,4,384]{2,1,0:T(4,128)S(1)}, f32[2,4,384,128]{3,2,1,0:T(8,128)}) %tuple.54, (s32[]{:T(128)}, s32[384]{0:T(512)S(1)}, s32[]{:T(128)}, ...), branch_computations={%region_5.5_spmd, %region_6.8_spmd} | conditional | flops 826940928 | bytes 40573572 | solution.py:146
  312.8 2.7 multiply_add_fusion
  320.4 14.7 %conditional.2 = ((f32[2,4,384]{2,1,0:T(4,128)S(1)}, f32[2,4,384]{2,1,0:T(4,128)S(1)}, f32[2,4,384,128]{3,2,1,0:T(8,128)})) conditional(s32[]{:T(128)} %convert_element_type.95, (f32[2,4,384]{2,1,0:T(4,128)S(1)}, f32[2,4,384]{2,1,0:T(4,128)S(1)}, f32[2,4,384,128]{3,2,1,0:T(8,128)}) %tuple.54, (s32[]{:T(128)}, s32[384]{0:T(512)S(1)}, s32[]{:T(128)}, ...), branch_computations={%region_5.5_spmd, %region_6.8_spmd} | conditional | flops 826940928 | bytes 40573572 | solution.py:146
  331.2 2.7 multiply_add_fusion
  338.8 14.7 %conditional.2 = ((f32[2,4,384]{2,1,0:T(4,128)S(1)}, f32[2,4,384]{2,1,0:T(4,128)S(1)}, f32[2,4,384,128]{3,2,1,0:T(8,128)})) conditional(s32[]{:T(128)} %convert_element_type.95, (f32[2,4,384]{2,1,0:T(4,128)S(1)}, f32[2,4,384]{2,1,0:T(4,128)S(1)}, f32[2,4,384,128]{3,2,1,0:T(8,128)}) %tuple.54, (s32[]{:T(128)}, s32[384]{0:T(512)S(1)}, s32[]{:T(128)}, ...), branch_computations={%region_5.5_spmd, %region_6.8_spmd} | conditional | flops 826940928 | bytes 40573572 | solution.py:146
  (147 shorter events, 112.7 us)
Async XLA Ops:
  7.2 127.1 %copy-start = (bf16[1,384,4096]{2,1,0:T(8,128)(2,1)S(1)}, bf16[1,384,4096]{2,1,0:T(8,128)(2,1)}, u32[]{:S(2)}) copy-start(bf16[1,384,4096]{2,1,0:T(8,128)(2,1)} %param.13) | copy-start | bytes 9437188
  7.2 95.3 %all-gather.3.cloned.1.call-start = ((), (), s32[]{:S(2)}) async-start(), calls=%async_computation.1 | async-start | bytes 12779520 | tf_op jit(solution)/shard_map/all_gather | solution.py:22
  9.0 218.6 %all-gather.5.cloned.1.call-start = ((), (), s32[]{:S(2)}) async-start(), calls=%async_computation.2 | async-start | bytes 3538944 | tf_op jit(solution)/shard_map/all_gather | solution.py:37
  9.1 7.9 %collective-permute-start = (bf16[512,4096]{1,0:T(8,128)(2,1)}, bf16[512,4096]{1,0:T(8,128)(2,1)}, u32[]{:S(2)}, u32[]{:S(2)}) collective-permute-start(bf16[512,4096]{1,0:T(8,128)(2,1)} %bitcast.155), channel_id=1, source_target_pairs={{0,8},{8,0},{1,9},{9,1},{2,10},{10,2},{3,11},{11,3},{4,12},{12,4},... | collective-permute-start | bytes 12582920 | tf_op jit(solution)/shard_map/ppermute | solution.py:92
  108.9 4.5 %copy-start.1 = (bf16[4,2,4,2,64,1536]{5,4,3,2,1,0:T(8,128)(2,1)}, bf16[4,2,4,2,64,1536]{5,4,3,2,1,0:T(8,128)(2,1)S(1)}, u32[]{:S(2)}) copy-start(bf16[4,2,4,2,64,1536]{5,4,3,2,1,0:T(8,128)(2,1)S(1)} %copy.79) | copy-start | bytes 37748740
  137.1 3.1 copy-start.5
  180.2 5.0 %copy-start.6 = (bf16[512,2,4,128]{0,3,2,1:T(8,128)(2,1)S(1)}, bf16[512,2,4,128]{0,3,2,1:T(8,128)(2,1)}, u32[]{:S(2)}) copy-start(bf16[512,2,4,128]{0,3,2,1:T(8,128)(2,1)} %fusion.42) | copy-start | bytes 3145732
  256.0 1.6 copy-start.2
  256.0 1.6 copy-start.3
  260.3 1.2 copy-start.4
  274.4 1.6 copy-start.2
  274.4 1.6 copy-start.3
  278.7 1.2 copy-start.4
  292.8 1.6 copy-start.2
  292.8 1.6 copy-start.3
  297.1 1.2 copy-start.4
  311.2 1.6 copy-start.2
  311.2 1.6 copy-start.3
  315.5 1.2 copy-start.4
  329.6 1.6 copy-start.2
  329.6 1.6 copy-start.3
  333.9 1.2 copy-start.4
  348.0 1.6 copy-start.2
  348.0 1.6 copy-start.3
  352.3 1.2 copy-start.4
Sparse Core Ops, SparseCore 0:
  11.4 91.0 all-gather.2
  142.6 70.6 all-gather.4

commit v2 on v0

v2 whole, which is shorter than its diff:
```python
import math

import jax
import jax.numpy as jnp
from jax import lax
from jax.experimental import pallas as pl
from jax.experimental.pallas import tpu as pltpu
from jax.sharding import PartitionSpec as P

HD = 128
HIDDEN = -1e30
EXP_SCALE = math.log2(math.e) / math.sqrt(HD)
VMEM = pltpu.VMEM


def torus_order():
    return [
        (x * 2 + y % 2) * 8 + z * 2 + y // 2 for x in range(4) for z in range(4) for y in range(4)
    ]


def blk_order():
    return [x * 2 + y_lo for y_lo in range(2) for x in range(4)]


def project_tile(tokens, weights):
    total = None
    for part in range(8):
        x, y_lo = part // 2, part % 2
        rows = weights[x, :, :, y_lo].reshape(512, weights.shape[-1])
        term = jnp.dot(
            tokens[:, 512 * part : 512 * (part + 1)], rows, preferred_element_type=jnp.float32
        )
        total = term if total is None else total + term
    return total.astype(jnp.bfloat16)


def long_kv_kernel(tokens, weights, out):
    out[...] = project_tile(tokens, weights)


def project_kernel(core, own, partner, long, weights, out_short, out_long):
    first = pl.multiple_of(core[0] * 512, 512)
    out_short[pl.ds(first, 512), :] = project_tile(own, weights)
    out_short[pl.ds(512 - first, 512), :] = project_tile(partner, weights)

    @pl.when(pl.program_id(0) >= 2)
    def _():
        out_long[...] = project_tile(long, weights)


WEIGHT_BLOCK = (4, 4, 2, 2, 64, 256)


def project_long_kv(long_rows, weights):
    return pl.pallas_call(
        long_kv_kernel,
        grid=(2,),
        in_specs=[
            pl.BlockSpec(memory_space=VMEM),
            pl.BlockSpec(WEIGHT_BLOCK, lambda n: (0, 0, 0, 0, 0, n)),
        ],
        out_specs=pl.BlockSpec((384, 256), lambda n: (0, n)),
        out_shape=jax.ShapeDtypeStruct((384, 512), jnp.bfloat16),
        compiler_params=pltpu.CompilerParams(vmem_limit_bytes=24 << 20),
        cost_estimate=pl.CostEstimate(
            flops=2 * 384 * 4096 * 512, bytes_accessed=8 << 20, transcendentals=0
        ),
    )(long_rows, weights)


def project_rest(core, own, partner, long_rows, weights):
    return pl.pallas_call(
        project_kernel,
        grid_spec=pltpu.PrefetchScalarGridSpec(
            num_scalar_prefetch=1,
            grid=(6,),
            in_specs=[
                pl.BlockSpec(memory_space=VMEM),
                pl.BlockSpec(memory_space=VMEM),
                pl.BlockSpec(memory_space=VMEM),
                pl.BlockSpec(WEIGHT_BLOCK, lambda n, core: (0, 0, 0, 0, 0, n)),
            ],
            out_specs=[
                pl.BlockSpec((1024, 256), lambda n, core: (0, n)),
                pl.BlockSpec((384, 256), lambda n, core: (0, jnp.maximum(n - 2, 0))),
            ],
        ),
        out_shape=[
            jax.ShapeDtypeStruct((1024, 1536), jnp.bfloat16),
            jax.ShapeDtypeStruct((384, 1024), jnp.bfloat16),
        ],
        compiler_params=pltpu.CompilerParams(vmem_limit_bytes=40 << 20),
        cost_estimate=pl.CostEstimate(
            flops=2 * 1408 * 4096 * 1536, bytes_accessed=24 << 20, transcendentals=0
        ),
    )(core, own, partner, long_rows, weights)


def softmax_rows(scores):
    scaled = scores * EXP_SCALE
    top = jnp.max(scaled, axis=-1, keepdims=True)
    return jnp.exp2(scaled - top)


QUERY_ROWS = 128


def short_kernel(seg_row, seg_col, queries, keys, values, out):
    for block in range(1024 // QUERY_ROWS):
        first = block * QUERY_ROWS
        start = max(0, first - 512)
        end = first + QUERY_ROWS
        width = end - start
        same = seg_col[first:end, 0:1] == seg_row[0:1, start:end]
        query_pos = first + lax.broadcasted_iota(jnp.int32, (QUERY_ROWS, width), 0)
        key_pos = start + lax.broadcasted_iota(jnp.int32, (QUERY_ROWS, width), 1)
        bias = jnp.where(same & (key_pos <= query_pos), 0.0, HIDDEN)
        key_rows = keys[start:end, :]
        value_rows = values[start:end, :]
        for head in range(4):
            scores = lax.dot_general(
                queries[first:end, head * HD : (head + 1) * HD],
                key_rows,
                (((1,), (1,)), ((), ())),
                preferred_element_type=jnp.float32,
            )
            exponentials = softmax_rows(scores + bias)
            totals = jnp.sum(exponentials, axis=-1, keepdims=True)
            mixed = jnp.dot(
                exponentials.astype(jnp.bfloat16), value_rows, preferred_element_type=jnp.float32
            )
            out[first:end, head * HD : (head + 1) * HD] = (mixed * (1.0 / totals)).astype(
                jnp.bfloat16
            )


def short_attention(segments, projected):
    seg_col = jnp.broadcast_to(segments.reshape(1024, 1), (1024, 128))
    return pl.pallas_call(
        short_kernel,
        grid=(2,),
        in_specs=[
            pl.BlockSpec((1, 1024), lambda g: (0, 0)),
            pl.BlockSpec((1024, 128), lambda g: (0, 0)),
            pl.BlockSpec((1024, 512), lambda g: (0, 1 + g)),
            pl.BlockSpec((1024, 128), lambda g: (0, g)),
            pl.BlockSpec((1024, 128), lambda g: (0, 2 + g)),
        ],
        out_specs=pl.BlockSpec((1024, 512), lambda g: (0, g)),
        out_shape=jax.ShapeDtypeStruct((1024, 1024), jnp.bfloat16),
        compiler_params=pltpu.CompilerParams(vmem_limit_bytes=24 << 20),
        cost_estimate=pl.CostEstimate(
            flops=8 * 1024 * 640 * 512, bytes_accessed=6 << 20, transcendentals=8 * 1024 * 640
        ),
    )(segments, seg_col, projected, projected, projected)


LONG_ROWS = 384


def long_kernel(place, queries, kv, out, top, total, mixed):
    block = place[0]
    length = place[1]
    first = block * LONG_ROWS
    live = first < length
    rows_shape = (LONG_ROWS, LONG_ROWS)

    def visit(index, head, diagonal):
        slot = index // 2 + 4 * (index % 2)
        at = pl.multiple_of(slot * LONG_ROWS, LONG_ROWS)
        group = head // 4
        key_rows = kv[pl.ds(at, LONG_ROWS), group * HD : (group + 1) * HD]
        value_rows = kv[pl.ds(at, LONG_ROWS), 256 + group * HD : 256 + (group + 1) * HD]
        scores = lax.dot_general(
            queries[:, head * HD : (head + 1) * HD],
            key_rows,
            (((1,), (1,)), ((), ())),
            preferred_element_type=jnp.float32,
        )
        scores = scores * EXP_SCALE
        key_pos = index * LONG_ROWS + lax.broadcasted_iota(jnp.int32, rows_shape, 1)
        visible = key_pos < length
        if diagonal:
            query_pos = first + lax.broadcasted_iota(jnp.int32, rows_shape, 0)
            visible = visible & (key_pos <= query_pos)
        scores = jnp.where(visible, scores, HIDDEN)
        old = top[head]
        new = jnp.maximum(old, jnp.max(scores, axis=-1, keepdims=True))
        rescale = jnp.exp2(old - new)
        exponentials = jnp.exp2(scores - new)
        top[head] = new
        total[head] = total[head] * rescale + jnp.sum(exponentials, axis=-1, keepdims=True)
        mixed[head] = mixed[head] * rescale + jnp.dot(
            exponentials.astype(jnp.bfloat16), value_rows, preferred_element_type=jnp.float32
        )

    @pl.when(live)
    def _():
        top[...] = jnp.full_like(top, HIDDEN)
        total[...] = jnp.zeros_like(total)
        mixed[...] = jnp.zeros_like(mixed)

        @pl.loop(0, block)
        def _(index):
            for head in range(8):
                visit(index, head, False)

        for head in range(8):
            visit(block, head, True)
        position = first + lax.broadcasted_iota(jnp.int32, (LONG_ROWS, HD), 0)
        for head in range(8):
            done = mixed[head] * (1.0 / total[head])
            out[:, head * HD : (head + 1) * HD] = jnp.where(position < length, done, 0.0).astype(
                jnp.bfloat16
            )

    @pl.when(jnp.logical_not(live))
    def _():
        out[...] = jnp.zeros_like(out)


def long_attention(place, queries, kv):
    return pl.pallas_call(
        long_kernel,
        in_specs=[
            pl.BlockSpec(memory_space=pltpu.SMEM),
            pl.BlockSpec(memory_space=VMEM),
            pl.BlockSpec(memory_space=VMEM),
        ],
        out_specs=pl.BlockSpec(memory_space=VMEM),
        out_shape=jax.ShapeDtypeStruct((LONG_ROWS, 1024), jnp.bfloat16),
        scratch_shapes=[
            VMEM((8, LONG_ROWS, 1), jnp.float32),
            VMEM((8, LONG_ROWS, 1), jnp.float32),
            VMEM((8, LONG_ROWS, HD), jnp.float32),
        ],
        compiler_params=pltpu.CompilerParams(vmem_limit_bytes=24 << 20),
        cost_estimate=pl.CostEstimate(
            flops=8 * 384 * 3072 * 512, bytes_accessed=6 << 20, transcendentals=8 * 384 * 3072
        ),
    )(place, queries, kv)


def local(short_tokens, short_segments, long_tokens, long_lengths, w_query, w_key, w_value):
    short_rows = short_tokens[0]
    long_rows = long_tokens[0]
    core = lax.axis_index("uly")
    partner_rows = lax.ppermute(short_rows, "uly", [(0, 1), (1, 0)])
    both = jnp.concatenate((w_key, w_value, w_query), axis=1)
    weights = lax.all_gather(
        both, ("blk", "dp"), axis=0, tiled=True, axis_index_groups=[torus_order()]
    ).reshape(4, 4, 2, 2, 64, 1536)
    long_kv = project_long_kv(long_rows, weights)
    kv = lax.all_gather(long_kv, "blk", axis=0, tiled=True, axis_index_groups=[blk_order()])
    core_index = core.astype(jnp.int32).reshape(1)
    projected, long_queries = project_rest(
        core_index, short_rows, partner_rows, long_rows, weights
    )
    attended = short_attention(short_segments, projected)
    mine = lax.dynamic_slice_in_dim(attended, core * 512, 512, axis=0)
    theirs = lax.dynamic_slice_in_dim(attended, 512 - core * 512, 512, axis=0)
    other = lax.ppermute(theirs, "uly", [(0, 1), (1, 0)])
    short_out = jnp.concatenate(
        [jnp.where(core == 0, mine, other), jnp.where(core == 0, other, mine)], axis=1
    )
    place = jnp.stack([lax.axis_index("blk").astype(jnp.int32), long_lengths[0]])
    long_out = long_attention(place, long_queries, kv)
    return short_out[None], long_out[None]


def solution(mesh):
    return jax.shard_map(
        local,
        mesh=mesh,
        in_specs=(
            P(("blk", "dp"), "uly", None),
            P(("blk", "dp"), None),
            P("dp", "blk", None),
            P("dp"),
            P(("blk", "dp"), "uly"),
            P(("blk", "dp"), "uly"),
            P(("blk", "dp"), "uly"),
        ),
        out_specs=(P(("blk", "dp"), "uly", None), P("dp", "blk", "uly")),
        check_vma=False,
    )
```

time: 613 us -> 217 us (0.35)
  the two profiles are of different devices: /device:TPU:71 before, /device:TPU:63 now
where the time goes in v2:
time: 217 us
  waiting for transfers between devices  94.6 us (44%)
  Pallas kernels  90.5 us (42%)
  between operations  14.8 us (7%)
  local copies, waits for them, and re-layouts  11.8 us (5%)
  other arithmetic  3.74 us (2%)
    all_gather x1, waiting for transfers between devices, local(): lax.all_gather(both, ('blk', 'dp'), axis=0, tiled=True, axis_index_groups...  92.8 us
    pallas_call x1, Pallas kernels, long_attention(): pl.pallas_call(long_kernel, in_specs=[pl.BlockSpec(memory_space=pltpu.SME...  48.2 us
    pallas_call x1, Pallas kernels, project_rest(): pl.pallas_call(project_kernel, grid_spec=pltpu.PrefetchScalarGridSpec(num...  21.3 us
    pallas_call x1, Pallas kernels, short_attention(): pl.pallas_call(short_kernel, grid=(2,), in_specs=[pl.BlockSpec((1, 1024),...  18 us
    unnamed x16, local copies, waits for them, and re-layouts  10.6 us
  transfers between devices with their start and end apart: 4, of which 2 were waited for; matrix products, arithmetic and copies ran while one was open for 2% of the time, Pallas kernels for 19%

profile of v2, /device:TPU:63, one launch (start us, length us, event | category | flops | bytes accessed | tf_op | source)
XLA Modules:
  0.0 217.1 jit_solution(3008284370280208525)
XLA Ops:
  7.2 0.0 all-gather.3.cloned.1.call-start
  7.2 1.6 pad_maximum_fusion
  8.8 0.0 all-gather.3.cloned.1.call-update
  8.8 0.0 all-gather.5.cloned.1.call-start
  8.9 0.8 collective-permute-start
  9.6 92.8 %all-gather.3.cloned.1.call-done = bf16[4096,1536]{1,0:T(8,128)(2,1)} async-done(((bf16[64,1536]{1,0:T(8,128)(2,1)}), bf16[4096,1536]{1,0:T(8,128)(2,1)}) %all-gather.3.cloned.1.call-update) | async-done | bytes 12582928 | tf_op jit(solution)/shard_map/all_gather | solution.py:251
  102.5 0.0 copy-start
  102.5 4.6 %copy-done = bf16[4096,1536]{1,0:T(8,128)(2,1)S(1)} copy-done((bf16[4096,1536]{1,0:T(8,128)(2,1)S(1)}, bf16[4096,1536]{1,0:T(8,128)(2,1)}, u32[]{:S(2)}) %copy-start) | copy-done | bytes 12582936
  107.0 0.0 copy-start.1
  107.0 1.9 copy-done.1
  108.9 3.0 %shard_map.88 = bf16[384,512]{1,0:T(8,128)(2,1)} custom-call(bf16[384,4096]{1,0:T(8,128)(2,1)S(1)} %bitcast.11, bf16[4,4,2,2,64,1536]{5,4,3,2,1,0:T(8,128)(2,1)S(1)} %bitcast.10), custom_call_target="tpu_custom_call" | custom-call | flops 1610612736 | bytes 8388608 | tf_op jit(solution)/shard_map/pallas_call | solution.py:56
  111.9 0.0 all-gather.5.cloned.1.call-update
  111.9 0.0 collective-permute-done.partner
  111.9 0.0 copy-done.2
  112.0 0.0 copy-start.4
  112.0 2.2 %copy-done.4 = bf16[1,512,4096]{2,1,0:T(8,128)(2,1)S(1)} copy-done((bf16[1,512,4096]{2,1,0:T(8,128)(2,1)S(1)}, bf16[1,512,4096]{2,1,0:T(8,128)(2,1)}, u32[]{:S(2)}) %copy-start.4) | copy-done | bytes 4194328
  114.1 21.3 %shard_map.86 = (bf16[1024,1536]{1,0:T(8,128)(2,1)S(1)}, bf16[384,1024]{1,0:T(8,128)(2,1)S(1)}) custom-call(s32[1]{0:T(128)} %bitcast.1.core, bf16[512,4096]{1,0:T(8,128)(2,1)S(1)} %bitcast.15, bf16[512,4096]{1,0:T(8,128)(2,1)} %collective-permute-done.partner, bf16[384,4096]{1,0:T(8,128)(2,1)S(1)} %bitcast.12, bf16[4,4,2,2,64,1536]{5,4,3,2,1,0:T(8,128)(2,1)} %bitcast.9), custom_call_target="tpu_custom_call" | custom-call | flops 17716740096 | bytes 25165824 | tf_op jit(solution)/shard_map/pallas_call | solution.py:73
  135.4 0.0 copy-start.6
  135.5 0.0 copy-done.3
  135.5 0.2 broadcast_in_dim.14.seg_col
  135.7 18.0 %shard_map.87 = bf16[1024,1024]{1,0:T(8,128)(2,1)S(1)} custom-call(s32[1,1024]{1,0:T(1,128)S(1)} %copy-done.3, s32[1024,128]{1,0:T(8,128)S(1)} %broadcast_in_dim.14.seg_col, bf16[1024,1536]{1,0:T(8,128)(2,1)S(1)} %get-tuple-element.4.queries.keys.values, bf16[1024,1536]{1,0:T(8,128)(2,1)S(1)} %get-tuple-element.4.queries.keys.values, ...), custom_call_target="tpu_custom_call" | custom-call | flops 2684354560 | bytes 6291456 | tf_op jit(solution)/shard_map/pallas_call | solution.py:140
  153.7 0.0 copy-done.6
  153.7 1.0 constant_dynamic-slice_fusion
  154.7 0.8 collective-permute-start.1
  156.2 0.1 pad_add_fusion.place
  156.3 1.8 collective-permute-done.1
  158.1 0.6 broadcast_select_fusion.1
  158.6 0.0 copy-start.7
  158.6 1.5 maximum_bitcast_fusion
  160.1 0.0 copy-done.7
  160.1 1.9 copy-done.5
  162.0 48.2 %shard_map.89 = bf16[384,1024]{1,0:T(8,128)(2,1)} custom-call(s32[2]{0:T(128)S(1)} %pad_add_fusion.place, bf16[384,1024]{1,0:T(8,128)(2,1)S(1)} %copy-done.7, bf16[3072,512]{1,0:T(8,128)(2,1)S(1)} %copy-done.5), custom_call_target="tpu_custom_call" | custom-call | flops 4831838208 | bytes 6291456 | tf_op jit(solution)/shard_map/pallas_call | solution.py:224
  (4 shorter events, 0.0 us)
Async XLA Ops:
  7.2 95.3 %all-gather.3.cloned.1.call-start = ((), (), s32[]{:S(2)}) async-start(), calls=%async_computation | async-start | bytes 12779520 | tf_op jit(solution)/shard_map/all_gather | solution.py:251
  8.8 151.3 %all-gather.5.cloned.1.call-start = ((), (), s32[]{:S(2)}) async-start(), calls=%async_computation.1 | async-start | bytes 3538944 | tf_op jit(solution)/shard_map/all_gather | solution.py:255
  8.9 103.1 %collective-permute-start = (bf16[512,4096]{1,0:T(8,128)(2,1)}, bf16[512,4096]{1,0:T(8,128)(2,1)}, u32[]{:S(2)}, u32[]{:S(2)}) collective-permute-start(bf16[512,4096]{1,0:T(8,128)(2,1)} %bitcast.14), channel_id=1, source_target_pairs={{0,8},{8,0},{1,9},{9,1},{2,10},{10,2},{3,11},{11,3},{4,12},{12,4},... | collective-permute-start | bytes 12582920 | tf_op jit(solution)/shard_map/ppermute | solution.py:249
  102.5 4.6 %copy-start = (bf16[4096,1536]{1,0:T(8,128)(2,1)S(1)}, bf16[4096,1536]{1,0:T(8,128)(2,1)}, u32[]{:S(2)}) copy-start(bf16[4096,1536]{1,0:T(8,128)(2,1)} %all-gather.3.cloned.1.call-done) | copy-start | bytes 37748740
  107.0 1.9 copy-start.1
  108.9 3.0 %copy-start.2 = (bf16[1,384,4096]{2,1,0:T(8,128)(2,1)S(1)}, bf16[1,384,4096]{2,1,0:T(8,128)(2,1)}, u32[]{:S(2)}) copy-start(bf16[1,384,4096]{2,1,0:T(8,128)(2,1)} %param.9) | copy-start | bytes 9437188
  112.0 2.2 %copy-start.4 = (bf16[1,512,4096]{2,1,0:T(8,128)(2,1)S(1)}, bf16[1,512,4096]{2,1,0:T(8,128)(2,1)}, u32[]{:S(2)}) copy-start(bf16[1,512,4096]{2,1,0:T(8,128)(2,1)} %param.7) | copy-start | bytes 12582916
  114.1 21.3 %copy-start.3 = (s32[1,1024]{1,0:T(1,128)S(1)}, s32[1,1024]{1,0:T(1,128)}, u32[]{:S(2)}) copy-start(s32[1,1024]{1,0:T(1,128)} %seg_row.1) | copy-start | bytes 12292
  135.4 18.2 %copy-start.6 = (bf16[384,1024]{1,0:T(8,128)(2,1)}, bf16[384,1024]{1,0:T(8,128)(2,1)S(1)}, u32[]{:S(2)}) copy-start(bf16[384,1024]{1,0:T(8,128)(2,1)S(1)} %get-tuple-element.5.queries) | copy-start | bytes 2359300
  154.7 3.3 %collective-permute-start.1 = (bf16[512,1024]{1,0:T(8,128)(2,1)}, bf16[512,1024]{1,0:T(8,128)(2,1)S(1)}, u32[]{:S(2)}, u32[]{:S(2)}) collective-permute-start(bf16[512,1024]{1,0:T(8,128)(2,1)} %constant_dynamic-slice_fusion), channel_id=1, source_target_pairs={{0,8},{8,0},{1,9},{9,1},{2,10},{10,2},{3,11},{11,3},{4,12},{12,4},... | collective-permute-start | bytes 3145736 | tf_op jit(solution)/shard_map/ppermute | solution.py:263
  158.6 1.5 copy-start.7
  160.1 1.9 copy-start.5
Sparse Core Ops, SparseCore 0:
  11.4 91.0 all-gather.2
  112.0 41.3 all-gather.4
